TPU v7x, 32 devices: a whole 2x2x4 slice. The times are simulated.
32 devices in a mesh: pop: 8 (over y, x, core), row: 4 (over z).
Axes of the slice: x: 2, y: 2, z: 4, core: 2. Of those that a mesh axis runs over, the one named last changes fastest.
Arguments:
- tokens: bfloat16 [384, 16, 4096], P('pop'), may hold values from -6 to 6
- weight: bfloat16 [14336, 4096], P('row', 'pop'), may hold values from -0.09375 to 0.09375
- bank_in: bfloat16 [4096, 128], P('row'), may hold values from -0.09375 to 0.09375
- bank_out: bfloat16 [14336, 128], P('row'), may hold values from -6 to 6
- fitness: int32 [384], P('pop'), may hold values from 0 to 191
- past_seeds: int32 [384, 2, 8], P('pop'), may hold values from 0 to 127
- new_seeds: int32 [384, 2, 8], P('pop'), may hold values from 0 to 127
Outputs:
- hidden: bfloat16 [384, 16, 14336], P('pop', None, 'row')
- new_weight: bfloat16 [14336, 4096], P('row', 'pop')
All inputs are finite; a program needn't handle non-finite values.
Results may differ from a plain program's by a relative error of at most 0.012.
Values may be sent and summed in bfloat16 or wider, within the bound.
No kernel may reach another device: no remote copies, remote signals or barrier semaphores. Data moves between devices by JAX's collectives and lax.ppermute only.
A program may use at most 128 MiB of HBM per device.

v0:
```python
import jax
import jax.numpy as jnp
from jax import lax
from jax.sharding import PartitionSpec as P

NOISE_SCALE = 0.1
STEP_SCALE = 0.03


def one_hots(seeds, width):
    levels = jnp.arange(width, dtype=jnp.int32)
    out_hits = (seeds[:, 0, :, None] == levels).astype(jnp.float32)
    in_hits = (seeds[:, 1, :, None] == levels).astype(jnp.float32)
    return (out_hits, in_hits)


def shards(tokens, weight, bank_in, bank_out, fitness, past_seeds, new_seeds):
    members = fitness.shape[0]
    overall = members * lax.axis_size("pop")
    width = bank_out.shape[1]
    everyone = lax.all_gather(fitness, "pop", axis=0, tiled=True)
    lower_count = jnp.sum((everyone[None, :] < fitness[:, None]).astype(jnp.float32), axis=1)
    equal_count = jnp.sum((everyone[None, :] == fitness[:, None]).astype(jnp.float32), axis=1)
    centered = (lower_count + 0.5 * (equal_count - 1.0)) / (overall - 1.0) - 0.5
    out_hits, in_hits = one_hots(past_seeds, width)
    local_coupling = STEP_SCALE * jnp.einsum("m,mki,mkj->ij", centered, out_hits, in_hits)
    coupling = lax.psum(local_coupling, "pop")
    full_in = lax.all_gather(bank_in, "row", axis=0, tiled=True)
    left_part = jnp.dot(bank_out.astype(jnp.float32), coupling, precision=lax.Precision.HIGHEST)
    features = tokens.shape[2]
    flat_tokens = tokens.reshape(members * tokens.shape[1], features)
    own_offset = lax.axis_index("pop") * weight.shape[1]
    columns = lax.dynamic_slice_in_dim(full_in, own_offset, weight.shape[1], 0).astype(jnp.float32)
    update = jnp.dot(left_part, columns.T, precision=lax.Precision.HIGHEST)
    new_weight = (weight.astype(jnp.float32) + update).astype(jnp.bfloat16)
    columns = flat_tokens
    base_part = lax.dot_general(
        columns,
        lax.all_gather(new_weight, "pop", axis=1, tiled=True),
        (((1,), (1,)), ((), ())),
        preferred_element_type=jnp.float32,
    )
    projected = jnp.dot(flat_tokens, full_in, preferred_element_type=jnp.float32).reshape(
        members, tokens.shape[1], width
    )
    hidden_hits, feature_hits = one_hots(new_seeds, width)
    mixing = jnp.einsum("mkb,mkc->mbc", feature_hits, hidden_hits)
    low_term = (NOISE_SCALE * jnp.einsum("mtb,mbc->mtc", projected, mixing)).astype(jnp.bfloat16)
    extra = lax.dot_general(
        low_term.reshape(flat_tokens.shape[0], width),
        bank_out,
        (((1,), (1,)), ((), ())),
        preferred_element_type=jnp.float32,
    )
    hidden = (
        (base_part + extra).astype(jnp.bfloat16).reshape(members, tokens.shape[1], weight.shape[0])
    )
    return (hidden, new_weight)


def solution(mesh):
    placed = (
        P("pop", None, None),
        P("row", "pop"),
        P("row", None),
        P("row", None),
        P("pop"),
        P("pop", None, None),
        P("pop", None, None),
    )
    return jax.shard_map(
        shards,
        mesh=mesh,
        in_specs=placed,
        out_specs=(P("pop", None, "row"), P("row", "pop")),
        check_vma=False,
    )
```

profile of v0, /device:TPU:0, one launch (start us, length us, event | category | flops | bytes accessed | tf_op | source)
XLA Modules:
  0.0 272.2 jit_solution(11762700354457997980)
XLA Ops:
  8.0 0.0 copy-start
  8.0 0.0 all-reduce.3.cloned.1.call-start
  8.1 1.3 dynamic-slice
  10.0 0.9 dynamic-update-slice
  10.9 9.5 %all-reduce = s32[384]{0:T(512)S(1)} all-reduce(s32[384]{0:T(512)S(1)} %dynamic-update-slice), channel_id=1, replica_groups=mesh['pop'=8,'row'=4] {'pop'}, use_global_device_ids=true, to_apply=%add | all-reduce | flops 384 | bytes 3072
  20.4 0.8 convert_reduce_fusion
  21.2 0.7 slice_bitcast_fusion.3
  21.9 0.1 copy.13
  22.0 0.1 copy.14
  22.1 1.0 fusion.16
  23.1 0.0 all-reduce.3.cloned.1.call-update
  23.2 0.0 all-gather.3.cloned.1.call-start
  23.2 0.5 all-gather.3.cloned.1.call-update
  23.7 0.0 all-gather.5.cloned.1.call-start
  23.8 52.4 %all-reduce.3.cloned.1.call-done = f32[128,128]{1,0:T(8,128)} async-done(((f32[128,128]{1,0:T(8,128)}), f32[128,128]{1,0:T(8,128)}) %all-reduce.3.cloned.1.call-update) | async-done | bytes 65552 | tf_op jit(solution)/shard_map/psum | solution.py:27
  76.2 0.0 copy-done
  76.2 1.8 fusion.31
  77.9 0.0 copy-start.1
  77.9 0.0 all-gather.3.cloned.1.call-done
  78.0 6.2 %add_convert_fusion = bf16[3584,512]{1,0:T(8,128)(2,1)} fusion(bf16[3584,512]{1,0:T(8,128)(2,1)} %param.8, f32[128,3584]{1,0:T(8,128)S(1)} %fusion.31, bf16[4096,128]{1,0:T(8,128)(2,1)} %all-gather.3.cloned.1.call-done, s32[]{:T(128)S(6)} %select_n.3), kind=kOutput, calls=%fused_computation.2 | convolution fusion | flops 2824077312 | bytes 9306116 | tf_op jit(solution)/shard_map/dot_general | solution.py:34
  84.2 0.0 all-gather.5.cloned.1.call-update
  84.2 0.0 copy-done.1
  84.2 0.1 copy.15
  84.3 0.1 copy.16
  84.4 6.3 %fusion.11 = bf16[48,16,128]{2,1,0:T(8,128)(2,1)S(1)} fusion(bf16[48,16,4096]{2,1,0:T(8,128)(2,1)} %param.7, bf16[4096,128]{1,0:T(8,128)(2,1)} %all-gather.3.cloned.1.call-done, s32[48,8]{1,0:T(8,128)S(1)} %copy.16, s32[48,8]{1,0:T(8,128)S(1)} %copy.15), kind=kOutput, calls=%fused_computation.7 | convolution fusion | flops 843350016 | bytes 7539712 | tf_op jit(solution)/shard_map/mtb,mbc->mtc/dot_general | solution.py:48
  90.7 141.8 %all-gather.5.cloned.1.call-done = bf16[3584,4096]{1,0:T(8,128)(2,1)} async-done(((bf16[3584,512]{1,0:T(8,128)(2,1)}), bf16[3584,4096]{1,0:T(8,128)(2,1)}) %all-gather.5.cloned.1.call-update) | async-done | bytes 29360144 | tf_op jit(solution)/shard_map/all_gather | solution.py:39
  232.5 28.2 %fusion.32 = f32[3584,768]{0,1:T(8,128)S(1)} fusion(bf16[3584,4096]{1,0:T(8,128)(2,1)} %all-gather.5.cloned.1.call-done, bf16[768,4096]{1,0:T(8,128)(2,1)} %bitcast.34), kind=kOutput, calls=%fused_computation.33 | convolution fusion | flops 22548578304 | bytes 46661632 | tf_op jit(solution)/shard_map/dot_general | solution.py:37
  260.7 4.0 %fusion = bf16[768,3584]{1,0:T(8,128)(2,1)} fusion(f32[3584,768]{0,1:T(8,128)S(1)} %fusion.32, bf16[768,128]{1,0:T(8,128)(2,1)S(1)} %bitcast.33, bf16[3584,128]{1,0:T(8,128)(2,1)S(1)} %copy-done), kind=kOutput, calls=%fused_computation.1 | convolution fusion | flops 710148096 | bytes 17629184 | tf_op jit(solution)/shard_map/dot_general | solution.py:49
  (3 shorter events, 0.0 us)
Async XLA Ops:
  8.0 68.2 %copy-start = (bf16[3584,128]{1,0:T(8,128)(2,1)S(1)}, bf16[3584,128]{1,0:T(8,128)(2,1)}, u32[]{:S(2)}) copy-start(bf16[3584,128]{1,0:T(8,128)(2,1)} %param.10) | copy-start | bytes 2752516
  8.0 68.1 %all-reduce.3.cloned.1.call-start = ((), (), s32[]{:S(2)}) async-start(), calls=%async_computation | async-start | bytes 131072 | tf_op jit(solution)/shard_map/psum | solution.py:27
  23.2 54.8 %all-gather.3.cloned.1.call-start = ((), (), s32[]{:S(2)}) async-start(), calls=%async_computation.1 | async-start | bytes 1310720 | tf_op jit(solution)/shard_map/all_gather | solution.py:28
  23.7 208.8 %all-gather.5.cloned.1.call-start = ((), (), s32[]{:S(2)}) async-start(), calls=%async_computation.2 | async-start | bytes 33030144 | tf_op jit(solution)/shard_map/all_gather | solution.py:39
  77.9 6.3 %copy-start.1 = (s32[48,2,8]{0,2,1:T(8,128)S(1)}, s32[48,2,8]{0,2,1:T(8,128)}, u32[]{:S(2)}) copy-start(s32[48,2,8]{0,2,1:T(8,128)} %param.13) | copy-start | bytes 9220
Sparse Core Ops, SparseCore 0:
  23.3 52.8 all-reduce.2
  84.3 148.1 all-gather.4
Sparse Core Ops, SparseCore 1:
  25.2 27.5 all-gather.2
where the time goes:
time: 272 us
  waiting for transfers between devices  195 us (72%)
  matrix products  47.6 us (18%)
  between operations  16.2 us (6%)
  blocking collectives  9.49 us (3%)
  local copies, waits for them, and re-layouts  3.23 us (1%)
    all_gather x1, waiting for transfers between devices, shards(): lax.all_gather(new_weight, 'pop', axis=1, tiled=True)  142 us
    psum x1, waiting for transfers between devices, shards(): coupling = lax.psum(local_coupling, 'pop')  52.4 us
    dot_general x1, matrix products, shards(): lax.dot_general(columns, lax.all_gather(new_weight, 'pop', axis=1, tiled=...  28.2 us
    unnamed x1, blocking collectives  9.49 us
    dot_general x1, matrix products, shards(): jnp.einsum('mtb,mbc->mtc', projected, mixing)  6.34 us
    dot_general x1, matrix products, shards(): update = jnp.dot(left_part, columns.T, precision=lax.Precision.HIGHEST)  6.22 us
  transfers between devices with their start and end apart: 3, of which 2 were waited for; matrix products, arithmetic and copies ran while one was open for 3% of the time, Pallas kernels for 0%

commit v1 on v0

--- a/solution.py
+++ b/solution.py
@@ -36,7 +36,7 @@
     columns = flat_tokens
     base_part = lax.dot_general(
         columns,
-        lax.all_gather(new_weight, "pop", axis=1, tiled=True),
+        jnp.concatenate(lax.all_gather(new_weight, "pop"), axis=1),
         (((1,), (1,)), ((), ())),
         preferred_element_type=jnp.float32,
     )

time: 272 us -> 303 us (1.11)
  local copies, waits for them, and re-layouts: 3.23 us -> 39.2 us
  waiting for transfers between devices: 195 us -> 189 us
    all_gather x0 -> x1, local copies, waits for them, and re-layouts: none -> 36 us  [shards(): lax.all_gather(new_weight, 'pop')]
    all_gather x1, waiting for transfers between devices: 142 us -> 136 us  [shards(): lax.all_gather(new_weight, 'pop')]
where the time goes in v1:
time: 303 us; the launch traced here: 302 us
  waiting for transfers between devices  189 us (62%)
  matrix products  47.3 us (16%)
  local copies, waits for them, and re-layouts  39.2 us (13%)
  between operations  16.2 us (5%)
  blocking collectives  9.49 us (3%)
    all_gather x1, waiting for transfers between devices, shards(): lax.all_gather(new_weight, 'pop')  136 us
    psum x1, waiting for transfers between devices, shards(): coupling = lax.psum(local_coupling, 'pop')  52.4 us
    all_gather x1, local copies, waits for them, and re-layouts, shards(): lax.all_gather(new_weight, 'pop')  36 us
    dot_general x1, matrix products, shards(): lax.dot_general(columns, jnp.concatenate(lax.all_gather(new_weight, 'pop'...  28 us
    unnamed x1, blocking collectives  9.49 us
    dot_general x1, matrix products, shards(): jnp.einsum('mtb,mbc->mtc', projected, mixing)  6.34 us
    dot_general x1, matrix products, shards(): update = jnp.dot(left_part, columns.T, precision=lax.Precision.HIGHEST)  6.22 us
  transfers between devices with their start and end apart: 3, of which 2 were waited for; matrix products, arithmetic and copies ran while one was open for 3% of the time, Pallas kernels for 0%

profile of v1, /device:TPU:0, one launch (start us, length us, event | category | flops | bytes accessed | tf_op | source)
XLA Modules:
  0.0 302.2 jit_solution(12458779925300625296)
XLA Ops:
  8.0 0.0 copy-start
  8.0 0.0 all-reduce.3.cloned.1.call-start
  8.1 1.3 dynamic-slice
  10.0 0.9 dynamic-update-slice
  10.9 9.5 %all-reduce = s32[384]{0:T(512)S(1)} all-reduce(s32[384]{0:T(512)S(1)} %dynamic-update-slice), channel_id=1, replica_groups=mesh['pop'=8,'row'=4] {'pop'}, use_global_device_ids=true, to_apply=%add | all-reduce | flops 384 | bytes 3072
  20.4 0.8 convert_reduce_fusion
  21.2 0.7 slice_bitcast_fusion.3
  21.9 0.1 copy.18
  22.0 0.1 copy.19
  22.1 1.0 fusion.16
  23.1 0.0 all-reduce.3.cloned.1.call-update
  23.2 0.0 all-gather.4.cloned.1.call-start
  23.2 0.5 all-gather.4.cloned.1.call-update
  23.7 0.0 all-gather.6.cloned.1.call-start
  23.8 52.4 %all-reduce.3.cloned.1.call-done = f32[128,128]{1,0:T(8,128)} async-done(((f32[128,128]{1,0:T(8,128)}), f32[128,128]{1,0:T(8,128)}) %all-reduce.3.cloned.1.call-update) | async-done | bytes 65552 | tf_op jit(solution)/shard_map/psum | solution.py:27
  76.2 0.0 copy-done
  76.2 1.8 fusion.31
  77.9 0.0 copy-start.1
  77.9 0.0 all-gather.4.cloned.1.call-done
  78.0 6.2 %add_convert_fusion = bf16[3584,512]{1,0:T(8,128)(2,1)} fusion(bf16[3584,512]{1,0:T(8,128)(2,1)} %param.8, f32[128,3584]{1,0:T(8,128)S(1)} %fusion.31, bf16[4096,128]{1,0:T(8,128)(2,1)} %all-gather.4.cloned.1.call-done, s32[]{:T(128)S(6)} %select_n.3), kind=kOutput, calls=%fused_computation.2 | convolution fusion | flops 2824077312 | bytes 9306116 | tf_op jit(solution)/shard_map/dot_general | solution.py:34
  84.2 0.0 all-gather.6.cloned.1.call-update
  84.2 0.0 copy-done.1
  84.2 0.1 copy.21
  84.3 0.1 copy.22
  84.4 6.3 %fusion.11 = bf16[48,16,128]{2,1,0:T(8,128)(2,1)S(1)} fusion(bf16[48,16,4096]{2,1,0:T(8,128)(2,1)} %param.7, bf16[4096,128]{1,0:T(8,128)(2,1)} %all-gather.4.cloned.1.call-done, s32[48,8]{1,0:T(8,128)S(1)} %copy.22, s32[48,8]{1,0:T(8,128)S(1)} %copy.21), kind=kOutput, calls=%fused_computation.7 | convolution fusion | flops 843350016 | bytes 7539712 | tf_op jit(solution)/shard_map/mtb,mbc->mtc/dot_general | solution.py:48
  90.7 136.0 %all-gather.6.cloned.1.call-done = bf16[28672,512]{1,0:T(8,128)(2,1)} async-done(((bf16[3584,512]{1,0:T(8,128)(2,1)}), bf16[28672,512]{1,0:T(8,128)(2,1)}) %all-gather.6.cloned.1.call-update) | async-done | bytes 29360144 | tf_op jit(solution)/shard_map/all_gather | solution.py:39
  226.7 36.0 %copy.20 = bf16[8,3584,512]{1,2,0:T(8,128)(2,1)} copy(bf16[8,3584,512]{2,1,0:T(8,128)(2,1)} %bitcast.36) | data formatting | bytes 58720256 | tf_op jit(solution)/shard_map/all_gather | solution.py:39
  262.7 28.0 %fusion.32 = f32[3584,768]{0,1:T(8,128)S(1)} fusion(bf16[768,4096]{1,0:T(8,128)(2,1)} %bitcast.40, bf16[3584,4096]{0,1:T(8,128)(2,1)} %bitcast.37), kind=kOutput, calls=%fused_computation.33 | convolution fusion | flops 22548578304 | bytes 46661632 | tf_op jit(solution)/shard_map/dot_general | solution.py:37
  290.7 4.0 %fusion = bf16[768,3584]{1,0:T(8,128)(2,1)} fusion(f32[3584,768]{0,1:T(8,128)S(1)} %fusion.32, bf16[768,128]{1,0:T(8,128)(2,1)S(1)} %bitcast.39, bf16[3584,128]{1,0:T(8,128)(2,1)S(1)} %copy-done), kind=kOutput, calls=%fused_computation.1 | convolution fusion | flops 710148096 | bytes 17629184 | tf_op jit(solution)/shard_map/dot_general | solution.py:49
  (3 shorter events, 0.0 us)
Async XLA Ops:
  8.0 68.2 %copy-start = (bf16[3584,128]{1,0:T(8,128)(2,1)S(1)}, bf16[3584,128]{1,0:T(8,128)(2,1)}, u32[]{:S(2)}) copy-start(bf16[3584,128]{1,0:T(8,128)(2,1)} %param.10) | copy-start | bytes 2752516
  8.0 68.1 %all-reduce.3.cloned.1.call-start = ((), (), s32[]{:S(2)}) async-start(), calls=%async_computation | async-start | bytes 131072 | tf_op jit(solution)/shard_map/psum | solution.py:27
  23.2 54.8 %all-gather.4.cloned.1.call-start = ((), (), s32[]{:S(2)}) async-start(), calls=%async_computation.1 | async-start | bytes 1310720 | tf_op jit(solution)/shard_map/all_gather | solution.py:28
  23.7 203.0 %all-gather.6.cloned.1.call-start = ((), (), s32[]{:S(2)}) async-start(), calls=%async_computation.2 | async-start | bytes 33030144 | tf_op jit(solution)/shard_map/all_gather | solution.py:39
  77.9 6.3 %copy-start.1 = (s32[48,2,8]{0,2,1:T(8,128)S(1)}, s32[48,2,8]{0,2,1:T(8,128)}, u32[]{:S(2)}) copy-start(s32[48,2,8]{0,2,1:T(8,128)} %param.13) | copy-start | bytes 9220
Sparse Core Ops, SparseCore 0:
  23.3 52.8 all-reduce.2
  84.3 142.3 all-gather.5
Sparse Core Ops, SparseCore 1:
  25.2 27.5 all-gather.3

commit v2 on v0

--- a/solution.py
+++ b/solution.py
@@ -24,7 +24,9 @@
     centered = (lower_count + 0.5 * (equal_count - 1.0)) / (overall - 1.0) - 0.5
     out_hits, in_hits = one_hots(past_seeds, width)
     local_coupling = STEP_SCALE * jnp.einsum("m,mki,mkj->ij", centered, out_hits, in_hits)
-    coupling = lax.psum(local_coupling, "pop")
+    coupling = local_coupling
+    for hop in (1, 2, 4):
+        coupling = coupling + lax.ppermute(coupling, "pop", [(dev, dev ^ hop) for dev in range(8)])
     full_in = lax.all_gather(bank_in, "row", axis=0, tiled=True)
     left_part = jnp.dot(bank_out.astype(jnp.float32), coupling, precision=lax.Precision.HIGHEST)
     features = tokens.shape[2]

time: 272 us -> 234 us (0.86)
  waiting for transfers between devices: 195 us -> 158 us
    psum x1 -> x0, waiting for transfers between devices: 52.4 us -> none  [shards(): coupling = lax.psum(local_coupling, 'pop')]
    ppermute x0 -> x3, waiting for transfers between devices: none -> 8.39 us  [shards(): lax.ppermute(coupling, 'pop', [(dev, dev ^ hop) for dev in range(8)])]
    all_gather x1, waiting for transfers between devices: 0.03 us -> 7.16 us  [shards(): full_in = lax.all_gather(bank_in, 'row', axis=0, tiled=True)]
  transfers between devices with their start and end apart: 3 -> 5, of which waited for: 2 -> 5; matrix products, arithmetic and copies ran while one was open for 3% -> 5% of each run, Pallas kernels for 0% -> 0%
where the time goes in v2:
time: 234 us
  waiting for transfers between devices  158 us (68%)
  matrix products  46.1 us (20%)
  between operations  14.8 us (6%)
  blocking collectives  9.49 us (4%)
  local copies, waits for them, and re-layouts  2.99 us (1%)
    all_gather x1, waiting for transfers between devices, shards(): lax.all_gather(new_weight, 'pop', axis=1, tiled=True)  142 us
    dot_general x1, matrix products, shards(): lax.dot_general(columns, lax.all_gather(new_weight, 'pop', axis=1, tiled=...  28.2 us
    unnamed x1, blocking collectives  9.49 us
    ppermute x3, waiting for transfers between devices, shards(): lax.ppermute(coupling, 'pop', [(dev, dev ^ hop) for dev in range(8)])  8.39 us
    all_gather x1, waiting for transfers between devices, shards(): full_in = lax.all_gather(bank_in, 'row', axis=0, tiled=True)  7.16 us
    dot_general x1, matrix products, shards(): jnp.einsum('mtb,mbc->mtc', projected, mixing)  6.34 us
    dot_general x1, matrix products, shards(): update = jnp.dot(left_part, columns.T, precision=lax.Precision.HIGHEST)  6.21 us
  transfers between devices with their start and end apart: 5, of which 5 were waited for; matrix products, arithmetic and copies ran while one was open for 5% of the time, Pallas kernels for 0%

profile of v2, /device:TPU:0, one launch (start us, length us, event | category | flops | bytes accessed | tf_op | source)
XLA Modules:
  0.0 233.9 jit_solution(1218226432475725347)
XLA Ops:
  7.2 0.0 copy-start
  7.2 0.0 all-gather.3.cloned.1.call-start
  7.2 0.7 all-gather.3.cloned.1.call-update
  7.9 0.0 all-gather.5.cloned.1.call-start
  8.0 1.2 dynamic-slice
  9.9 0.9 dynamic-update-slice
  10.7 9.5 %all-reduce = s32[384]{0:T(512)S(1)} all-reduce(s32[384]{0:T(512)S(1)} %dynamic-update-slice), channel_id=1, replica_groups=mesh['pop'=8,'row'=4] {'pop'}, use_global_device_ids=true, to_apply=%add | all-reduce | flops 384 | bytes 3072
  20.2 0.8 convert_reduce_fusion
  21.1 0.7 slice_bitcast_fusion.3
  21.8 0.4 fusion.16
  22.2 0.1 collective-permute-start
  22.3 1.2 collective-permute-done
  23.5 0.9 collective-permute-start.1
  24.4 3.4 %collective-permute-done.1 = f32[128,128]{1,0:T(8,128)S(1)} collective-permute-done((f32[128,128]{1,0:T(8,128)S(1)}, f32[128,128]{1,0:T(8,128)S(1)}, u32[]{:S(2)}, u32[]{:S(2)}) %collective-permute-start.1) | collective-permute-done | bytes 65568 | tf_op jit(solution)/shard_map/ppermute | solution.py:29
  27.9 0.6 collective-permute-start.2
  28.4 3.7 %collective-permute-done.2 = f32[128,128]{1,0:T(8,128)S(1)} collective-permute-done((f32[128,128]{1,0:T(8,128)S(1)}, f32[128,128]{1,0:T(8,128)S(1)}, u32[]{:S(2)}, u32[]{:S(2)}) %collective-permute-start.2) | collective-permute-done | bytes 65568 | tf_op jit(solution)/shard_map/ppermute | solution.py:29
  32.2 0.0 copy-done
  32.2 0.9 fusion.29
  33.1 0.0 copy-start.1
  33.1 7.2 %all-gather.3.cloned.1.call-done = bf16[4096,128]{1,0:T(8,128)(2,1)} async-done(((bf16[1024,128]{1,0:T(8,128)(2,1)}), bf16[4096,128]{1,0:T(8,128)(2,1)}) %all-gather.3.cloned.1.call-update) | async-done | bytes 1048592 | tf_op jit(solution)/shard_map/all_gather | solution.py:30
  40.3 6.2 %add_convert_fusion = bf16[3584,512]{1,0:T(8,128)(2,1)} fusion(bf16[3584,512]{1,0:T(8,128)(2,1)} %param.8, f32[128,3584]{1,0:T(8,128)S(1)} %fusion.29, bf16[4096,128]{1,0:T(8,128)(2,1)} %all-gather.3.cloned.1.call-done, s32[]{:T(128)S(6)} %select_n.3), kind=kOutput, calls=%fused_computation.2 | convolution fusion | flops 2824077312 | bytes 9306116 | tf_op jit(solution)/shard_map/dot_general | solution.py:36
  46.5 0.0 all-gather.5.cloned.1.call-update
  46.5 0.0 copy-done.1
  46.6 0.1 copy.11
  46.6 0.1 copy.12
  46.7 6.3 %fusion.11 = bf16[48,16,128]{2,1,0:T(8,128)(2,1)S(1)} fusion(bf16[48,16,4096]{2,1,0:T(8,128)(2,1)} %param.7, bf16[4096,128]{1,0:T(8,128)(2,1)} %all-gather.3.cloned.1.call-done, s32[48,8]{1,0:T(8,128)S(1)} %copy.12, s32[48,8]{1,0:T(8,128)S(1)} %copy.11), kind=kOutput, calls=%fused_computation.7 | convolution fusion | flops 843350016 | bytes 7539712 | tf_op jit(solution)/shard_map/mtb,mbc->mtc/dot_general | solution.py:50
  53.1 141.8 %all-gather.5.cloned.1.call-done = bf16[3584,4096]{1,0:T(8,128)(2,1)} async-done(((bf16[3584,512]{1,0:T(8,128)(2,1)}), bf16[3584,4096]{1,0:T(8,128)(2,1)}) %all-gather.5.cloned.1.call-update) | async-done | bytes 29360144 | tf_op jit(solution)/shard_map/all_gather | solution.py:41
  194.8 28.2 %fusion.33 = f32[3584,768]{0,1:T(8,128)S(1)} fusion(bf16[3584,4096]{1,0:T(8,128)(2,1)} %all-gather.5.cloned.1.call-done, bf16[768,4096]{1,0:T(8,128)(2,1)} %bitcast.33), kind=kOutput, calls=%fused_computation.34 | convolution fusion | flops 22548578304 | bytes 46661632 | tf_op jit(solution)/shard_map/dot_general | solution.py:39
  223.0 4.0 %fusion = bf16[768,3584]{1,0:T(8,128)(2,1)} fusion(f32[3584,768]{0,1:T(8,128)S(1)} %fusion.33, bf16[768,128]{1,0:T(8,128)(2,1)S(1)} %bitcast.32, bf16[3584,128]{1,0:T(8,128)(2,1)S(1)} %copy-done), kind=kOutput, calls=%fused_computation.1 | convolution fusion | flops 710148096 | bytes 17629184 | tf_op jit(solution)/shard_map/dot_general | solution.py:51
  (5 shorter events, 0.0 us)
Async XLA Ops:
  7.2 25.0 %copy-start = (bf16[3584,128]{1,0:T(8,128)(2,1)S(1)}, bf16[3584,128]{1,0:T(8,128)(2,1)}, u32[]{:S(2)}) copy-start(bf16[3584,128]{1,0:T(8,128)(2,1)} %param.10) | copy-start | bytes 2752516
  7.2 33.1 %all-gather.3.cloned.1.call-start = ((), (), s32[]{:S(2)}) async-start(), calls=%async_computation | async-start | bytes 1310720 | tf_op jit(solution)/shard_map/all_gather | solution.py:30
  7.9 186.9 %all-gather.5.cloned.1.call-start = ((), (), s32[]{:S(2)}) async-start(), calls=%async_computation.1 | async-start | bytes 33030144 | tf_op jit(solution)/shard_map/all_gather | solution.py:41
  22.2 1.3 collective-permute-start
  23.5 4.3 %collective-permute-start.1 = (f32[128,128]{1,0:T(8,128)S(1)}, f32[128,128]{1,0:T(8,128)S(1)}, u32[]{:S(2)}, u32[]{:S(2)}) collective-permute-start(f32[128,128]{1,0:T(8,128)S(1)} %add.24), channel_id=1, source_target_pairs={{0,8},{4,12},{8,0},{12,4},{16,24},{20,28},{24,16},{28,20},{1,9},{5... | collective-permute-start | bytes 196616 | tf_op jit(solution)/shard_map/ppermute | solution.py:29
  27.9 4.3 %collective-permute-start.2 = (f32[128,128]{1,0:T(8,128)S(1)}, f32[128,128]{1,0:T(8,128)S(1)}, u32[]{:S(2)}, u32[]{:S(2)}) collective-permute-start(f32[128,128]{1,0:T(8,128)S(1)} %add.25), channel_id=1, source_target_pairs={{0,16},{4,20},{8,24},{12,28},{16,0},{20,4},{24,8},{28,12},{1,17},{... | collective-permute-start | bytes 196616 | tf_op jit(solution)/shard_map/ppermute | solution.py:29
  33.1 13.4 %copy-start.1 = (s32[48,2,8]{0,2,1:T(8,128)S(1)}, s32[48,2,8]{0,2,1:T(8,128)}, u32[]{:S(2)}) copy-start(s32[48,2,8]{0,2,1:T(8,128)} %param.13) | copy-start | bytes 9220
Sparse Core Ops, SparseCore 0:
  9.6 30.6 all-gather.2
  46.7 148.1 all-gather.4
